TPU v7x, 8 devices: a whole 2x2x1 slice. The times are simulated.
8 devices in a mesh: rep: 1 (over z), pp: 8 (over x, y, core).
Axes of the slice: x: 2, y: 2, z: 1, core: 2. Of those that a mesh axis runs over, the one named last changes fastest.
Arguments:
- x: bfloat16 [16, 512, 512], P('rep')
- dy: bfloat16 [16, 512, 512], P('rep')
- w_gate: bfloat16 [8, 512, 1792], P('pp')
- w_up: bfloat16 [8, 512, 1792], P('pp')
- w_down: bfloat16 [8, 1792, 512], P('pp')
Outputs:
- output 1: bfloat16 [8, 512, 1792], P(('rep', 'pp'))
- output 2: bfloat16 [8, 512, 1792], P(('rep', 'pp'))
- output 3: bfloat16 [8, 1792, 512], P(('rep', 'pp'))
All inputs are finite; a program needn't handle non-finite values.
Results may differ from a plain program's by a relative error of at most 0.029.
Values are sent between devices in bfloat16 or wider.
A program may use at most 2 GiB of HBM per device.

v0:
```python
import jax
import jax.numpy as jnp
from jax import lax
from jax.sharding import PartitionSpec as P

NAMES = ("w_gate", "w_up", "w_down")


def matmul(a, w):
    return jnp.dot(a, w, preferred_element_type=jnp.float32).astype(jnp.bfloat16)


def normed(h):
    wide = h.astype(jnp.float32)
    scale = lax.rsqrt(jnp.mean(wide**2, -1, keepdims=True) + 1e-6)
    return (wide * scale).astype(jnp.bfloat16)


def layer(h, w):
    a = normed(h)
    gate = jnp.dot(a, w["w_gate"], preferred_element_type=jnp.float32)
    up = jnp.dot(a, w["w_up"], preferred_element_type=jnp.float32)
    return h + matmul((jax.nn.silu(gate) * up).astype(jnp.bfloat16), w["w_down"])


def stage(weights, h):
    for number in range(weights["w_gate"].shape[0]):
        h = layer(h, {name: w[number] for name, w in weights.items()})
    return h


def solution(mesh):
    stages = mesh.shape["pp"]
    onward = [(i, i + 1) for i in range(stages - 1)]
    back_again = [(i + 1, i) for i in range(stages - 1)]

    def step(x, dy, *arrays):
        weights = dict(zip(NAMES, arrays, strict=True))
        micro, me = x.shape[0], lax.axis_index("pp")
        kept, came = jnp.zeros_like(x), jnp.zeros_like(x[0])
        for t in range(micro + stages - 1):
            number = jnp.clip(t - me, 0, micro - 1)
            at_work = (t >= me) & (t - me < micro)
            h = jnp.where(me == 0, x[min(t, micro - 1)], came)
            was = lax.dynamic_index_in_dim(kept, number, 0, keepdims=False)
            kept = lax.dynamic_update_index_in_dim(kept, jnp.where(at_work, h, was), number, 0)
            came = lax.ppermute(stage(weights, h), "pp", onward)
        total = {name: jnp.zeros(w.shape, jnp.float32) for name, w in weights.items()}
        came, behind = jnp.zeros_like(x[0]), stages - 1 - me
        for t in range(micro + stages - 1):
            number = jnp.clip(t - behind, 0, micro - 1)
            at_work = (t >= behind) & (t - behind < micro)
            by_y = jnp.where(behind == 0, dy[min(t, micro - 1)], came)
            _, back = jax.vjp(stage, weights, lax.dynamic_index_in_dim(kept, number, 0, keepdims=False))
            by_w, by_h = back(by_y)
            total = {name: total[name] + jnp.where(at_work, by_w[name].astype(jnp.float32), 0.0) for name in NAMES}
            came = lax.ppermute(by_h, "pp", back_again)
        return tuple(total[name].astype(jnp.bfloat16) for name in NAMES)

    return jax.shard_map(
        step,
        mesh=mesh,
        in_specs=(P("rep", None, None),) * 2 + (P("pp", None, None),) * 3,
        out_specs=(P(("rep", "pp"), None, None),) * 3,
        check_vma=False,
    )
```

profile of v0, /device:TPU:3, one launch (start us, length us, event | category | flops | bytes accessed | tf_op | source)
XLA Modules:
  0.0 1174.1 jit_solution(5845683233719926461)
XLA Ops:
  6.3 5.5 fusion.812
  15.5 6.1 collective-permute-done
  25.9 5.3 fusion.809
  31.3 4.4 collective-permute-start.1
  35.7 6.1 collective-permute-done.1
  46.1 5.4 fusion.806
  51.4 4.4 collective-permute-start.2
  55.8 6.1 collective-permute-done.2
  66.2 6.2 fusion.803
  72.4 4.6 collective-permute-start.3
  77.0 5.9 collective-permute-done.3
  87.1 6.2 fusion.800
  93.3 4.4 collective-permute-start.4
  97.7 6.1 collective-permute-done.4
  108.9 6.3 fusion.797
  115.2 4.4 collective-permute-start.5
  119.6 6.1 collective-permute-done.5
  130.8 6.3 fusion.794
  137.1 4.4 collective-permute-start.6
  141.5 6.1 collective-permute-done.6
  152.7 6.3 fusion.791
  159.0 4.8 collective-permute-start.7
  163.8 6.2 collective-permute-done.7
  175.1 6.3 fusion.788
  185.4 7.5 collective-permute-done.8
  197.9 6.3 fusion.785
  207.3 8.3 collective-permute-done.9
  220.8 6.3 fusion.782
  244.2 6.4 fusion.779
  256.5 5.1 collective-permute-done.11
  266.9 6.4 fusion.776
  289.1 6.2 fusion.773
  310.9 6.2 fusion.770
  333.6 6.4 fusion.767
  356.6 6.4 fusion.764
  379.4 6.4 fusion.761
  401.6 6.2 fusion.758
  423.4 6.2 fusion.755
  445.3 6.2 fusion.752
  458.5 4.4 collective-permute-done.20
  467.2 6.2 fusion.749
  479.8 4.9 collective-permute-done.21
  507.8 6.3 fusion.1025
  516.0 9.9 collective-permute-start.22
  1071.2 5.2 collective-permute-done.42
  1108.8 21.0 %fusion.393 = bf16[1,512,1792]{2,1,0:T(8,128)(2,1)} fusion(pred[]{:T(512)S(6)} %and.184, bf16[512,1792]{1,0:T(8,128)(2,1)} %convolution_convert_fusion.23, pred[]{:T(512)S(6)} %and.183, bf16[512,1792]{1,0:T(8,128)(2,1)} %convolution_convert_fusion.24, pred[]{:T(512)S(6)} %and.182, bf16[512,1792]{1,0:T(8,128)(2,1)} %convolution_convert_fusion.25, ...), kind=kOutput, calls=%fused_computation.620 | convolution fusion | flops 1010040832 | bytes 48236572 | tf_op jit(solution)/shard_map/transpose(jvp())/dot_general | solution.py:22
  1129.9 22.4 %fusion.392 = bf16[1,512,1792]{2,1,0:T(8,128)(2,1)} fusion(pred[]{:T(512)S(6)} %and.184, bf16[512,1792]{1,0:T(8,128)(2,1)} %convolution_convert_fusion.46, pred[]{:T(512)S(6)} %and.183, bf16[512,1792]{1,0:T(8,128)(2,1)} %convolution_convert_fusion.48, pred[]{:T(512)S(6)} %and.182, bf16[512,1792]{1,0:T(8,128)(2,1)} %convolution_convert_fusion.50, ...), kind=kOutput, calls=%fused_computation.619 | convolution fusion | flops 1014628352 | bytes 51906588 | tf_op jit(solution)/shard_map/transpose(jvp())/dot_general | solution.py:21
  1152.2 21.4 %fusion.394 = bf16[1,1792,512]{2,1,0:T(8,128)(2,1)} fusion(pred[]{:T(512)S(6)} %and.184, bf16[1792,512]{1,0:T(8,128)(2,1)} %convolution_convert_fusion.1, pred[]{:T(512)S(6)} %and.183, bf16[1792,512]{1,0:T(8,128)(2,1)} %convolution_convert_fusion.2, pred[]{:T(512)S(6)} %and.182, bf16[1792,512]{1,0:T(8,128)(2,1)} %convolution_convert_fusion.3, ...), kind=kOutput, calls=%fused_computation.621 | convolution fusion | flops 1009516544 | bytes 50593816 | tf_op jit(solution)/shard_map/transpose(jvp())/dot_general | solution.py:10
  (676 shorter events, 837.9 us)
Async XLA Ops:
  11.8 9.8 collective-permute-start
  31.3 10.5 collective-permute-start.1
  51.4 10.5 collective-permute-start.2
  72.4 10.5 collective-permute-start.3
  93.3 10.5 collective-permute-start.4
  115.2 10.5 collective-permute-start.5
  137.1 10.5 collective-permute-start.6
  159.0 11.0 collective-permute-start.7
  181.5 11.4 collective-permute-start.8
  204.2 11.3 collective-permute-start.9
  227.2 11.9 %collective-permute-start.10 = (bf16[512,512]{1,0:T(8,128)(2,1)}, bf16[512,512]{1,0:T(8,128)(2,1)S(1)}, u32[]{:S(2)}, u32[]{:S(2)}) collective-permute-start(bf16[512,512]{1,0:T(8,128)(2,1)} %fusion.782), channel_id=1, source_target_pairs={{0,1},{1,2},{2,3},{3,4},{4,5},{5,6},{6,7}} | collective-permute-start | bytes 1572872 | tf_op jit(solution)/shard_map/ppermute | solution.py:47
  250.5 11.2 collective-permute-start.11
  273.3 11.4 collective-permute-start.12
  295.3 11.4 collective-permute-start.13
  317.2 11.4 collective-permute-start.14
  340.1 11.4 collective-permute-start.15
  363.0 11.4 collective-permute-start.16
  385.9 11.4 collective-permute-start.17
  407.8 11.4 collective-permute-start.18
  429.6 11.4 collective-permute-start.19
  451.5 11.4 collective-permute-start.20
  473.4 11.4 collective-permute-start.21
  514.2 72.7 %copy-start.78 = (f32[512]{0:T(512)}, f32[512]{0:T(512)S(1)}, u32[]{:S(2)}) copy-start(f32[512]{0:T(512)S(1)} %get-tuple-element.7) | copy-start | bytes 6148
  514.3 68.4 %copy-start.46 = (f32[512]{0:T(512)}, f32[512]{0:T(512)S(1)}, u32[]{:S(2)}) copy-start(f32[512]{0:T(512)S(1)} %fusion.1428) | copy-start | bytes 6148
  514.3 64.4 %copy-start.50 = (f32[512]{0:T(512)}, f32[512]{0:T(512)S(1)}, u32[]{:S(2)}) copy-start(f32[512]{0:T(512)S(1)} %fusion.1427) | copy-start | bytes 6148
  514.3 60.3 %copy-start.52 = (f32[512]{0:T(512)}, f32[512]{0:T(512)S(1)}, u32[]{:S(2)}) copy-start(f32[512]{0:T(512)S(1)} %fusion.1426) | copy-start | bytes 6148
  516.0 75.1 %collective-permute-start.22 = (bf16[512,512]{1,0:T(8,128)(2,1)S(1)}, bf16[512,512]{1,0:T(8,128)(2,1)S(1)}, u32[]{:S(2)}, u32[]{:S(2)}) collective-permute-start(bf16[512,512]{1,0:T(8,128)(2,1)S(1)} %fusion.1146), channel_id=1, source_target_pairs={{1,0},{2,1},{3,2},{4,3},{5,4},{6,5},{7,6}} | collective-permute-start | bytes 1572872 | tf_op jit(solution)/shard_map/ppermute | solution.py:57
  611.4 10.5 collective-permute-start.23
  634.1 10.5 collective-permute-start.24
  656.6 10.5 collective-permute-start.25
  679.2 10.8 collective-permute-start.26
  703.0 11.1 collective-permute-start.27
  727.1 10.8 collective-permute-start.28
  750.8 10.9 collective-permute-start.29
  774.6 10.6 collective-permute-start.30
  798.2 10.5 collective-permute-start.31
  821.7 10.7 collective-permute-start.32
  845.4 10.8 collective-permute-start.33
  869.2 10.5 collective-permute-start.34
  892.6 10.5 collective-permute-start.35
  916.0 10.8 collective-permute-start.36
  939.8 10.9 collective-permute-start.37
  963.6 10.6 collective-permute-start.38
  987.2 10.5 collective-permute-start.39
  1010.7 10.7 collective-permute-start.40
  1034.4 10.8 collective-permute-start.41
  1066.0 10.5 collective-permute-start.42
  1092.9 13.5 %collective-permute-start.43 = (bf16[512,512]{1,0:T(8,128)(2,1)S(1)}, bf16[512,512]{1,0:T(8,128)(2,1)S(1)}, u32[]{:S(2)}, u32[]{:S(2)}) collective-permute-start(bf16[512,512]{1,0:T(8,128)(2,1)S(1)} %fusion.1125), channel_id=1, source_target_pairs={{1,0},{2,1},{3,2},{4,3},{5,4},{6,5},{7,6}} | collective-permute-start | bytes 1572872 | tf_op jit(solution)/shard_map/ppermute | solution.py:57
  (111 other events, 982.9 us)
where the time goes:
time: 1190 us; the launch traced here: 1170 us
  matrix products  763 us (64%)
  starting transfers between devices  139 us (12%)
  waiting for transfers between devices  115 us (10%)
  other arithmetic  96.3 us (8%)
  local copies, waits for them, and re-layouts  56.9 us (5%)
    dot_general x90, matrix products, layer(): gate = jnp.dot(a, w['w_gate'], preferred_element_type=jnp.float32)  266 us
    dot_general x68, matrix products, layer(): up = jnp.dot(a, w['w_up'], preferred_element_type=jnp.float32)  250 us
    dot_general x68, matrix products, matmul(): jnp.dot(a, w, preferred_element_type=jnp.float32).astype(jnp.bfloat16)  246 us
    ppermute x22, waiting for transfers between devices, step(): came = lax.ppermute(stage(weights, h), 'pp', onward)  107 us
    ppermute x22, starting transfers between devices, step(): came = lax.ppermute(by_h, 'pp', back_again)  72.8 us
    ppermute x22, starting transfers between devices, step(): came = lax.ppermute(stage(weights, h), 'pp', onward)  66.4 us
    dynamic_update_slice x23, other arithmetic, step(): lax.dynamic_update_index_in_dim(kept, jnp.where(at_work, h, was), number, 0)  33.3 us
    dynamic_slice x22, local copies, waits for them, and re-layouts, step(): was = lax.dynamic_index_in_dim(kept, number, 0, keepdims=False)  30.9 us
  transfers between devices with their start and end apart: 44, of which 27 were waited for; matrix products, arithmetic and copies ran while one was open for 25% of the time, Pallas kernels for 0%

commit v1 on v0

v1 whole, which is shorter than its diff:
```python
import functools

import jax
import jax.numpy as jnp
from jax import lax
from jax.experimental import pallas as pl
from jax.experimental.pallas import tpu as pltpu
from jax.sharding import PartitionSpec as P

BF, F32 = jnp.bfloat16, jnp.float32
LEAD = (12, 11, 10, 8, 6, 4, 2, 0)
LAG = (1, 2, 3, 4, 5, 6, 6, 6)
TILE = 256
PARTS = 2
NN = (((1,), (0,)), ((), ()))
NT = (((1,), (1,)), ((), ()))


def dot(a, b, dims=NN):
    return lax.dot_general(a, b, dims, preferred_element_type=F32)


def scaled(h):
    wide = h.astype(F32)
    return wide, lax.rsqrt(jnp.mean(wide * wide, -1, keepdims=True) + 1e-6)


def tiles(ff):
    return [pl.ds(n, TILE) for n in range(0, ff, TILE)]


def pick(me, values):
    out = jnp.int32(values[0])
    for i in range(1, len(values)):
        out = jnp.where(me == i, jnp.int32(values[i]), out)
    return out


def kernel(stages, x, dy, wg_in, wu_in, wd_in, og, ou, od, gu_all, s_all, *scratch):
    (hb, db, wg, wu, wd, acc, gu, gu_in, s_out, s_in, ys, dhs, at, dyt,
     h_sem, d_sem, y_sent, dh_sent, w_sem, gu_sem, gu_in_sem, s_sem, s_in_sem, o_sem) = scratch
    micro, tokens, _ = hb.shape
    ff = wg.shape[1]
    rows = tokens // PARTS
    last = stages - 1
    me = lax.axis_index("pp")
    lead, lag = pick(me, LEAD), pick(me, LAG)
    parts = [pl.ds(p * rows, rows) for p in range(PARTS)]

    weights = [pltpu.make_async_copy(a, b, w_sem.at[j]) for j, (a, b) in enumerate(((wg_in, wg), (wu_in, wu), (wd_in, wd)))]
    for copy in weights:
        copy.start()

    @pl.when(me == 0)
    def _():
        for m in range(micro):
            for p, r in enumerate(parts):
                pltpu.make_async_copy(x.at[m, r], hb.at[m, r], h_sem.at[m, p]).start()

    @pl.when(me == last)
    def _():
        for m in range(micro):
            for p, r in enumerate(parts):
                pltpu.make_async_copy(dy.at[m, r], db.at[m, r], d_sem.at[m, p]).start()

    barrier = pltpu.get_barrier_semaphore()

    @pl.when(me > 0)
    def _():
        pl.semaphore_signal(barrier, inc=1, device_id={"pp": me - 1}, device_id_type=pl.DeviceIdType.MESH)

    @pl.when(me < last)
    def _():
        pl.semaphore_signal(barrier, inc=1, device_id={"pp": me + 1}, device_id_type=pl.DeviceIdType.MESH)

    acc[...] = jnp.zeros_like(acc)

    pl.semaphore_wait(barrier, (me > 0).astype(jnp.int32) + (me < last).astype(jnp.int32))

    for copy in weights:
        copy.wait()

    def onward(m, p):
        r = parts[p]
        return pltpu.make_async_remote_copy(
            src_ref=ys.at[m % 2, r], dst_ref=hb.at[m, r], send_sem=y_sent.at[m % 2, p], recv_sem=h_sem.at[m, p],
            device_id={"pp": me + 1}, device_id_type=pl.DeviceIdType.MESH)

    def back_again(m, p):
        r = parts[p]
        return pltpu.make_async_remote_copy(
            src_ref=dhs.at[m % 2, r], dst_ref=db.at[m, r], send_sem=dh_sent.at[m % 2, p], recv_sem=d_sem.at[m, p],
            device_id={"pp": me - 1}, device_id_type=pl.DeviceIdType.MESH)

    def h_came(m, p):
        r = parts[p]
        return pltpu.make_async_copy(x.at[m, r], hb.at[m, r], h_sem.at[m, p])

    def d_came(m, p):
        r = parts[p]
        return pltpu.make_async_copy(dy.at[m, r], db.at[m, r], d_sem.at[m, p])

    def gu_out(m):
        return [pltpu.make_async_copy(gu.at[j], gu_all.at[m, j], gu_sem.at[j]) for j in range(2)]

    def gu_back(m):
        return [pltpu.make_async_copy(gu_all.at[m, j], gu_in.at[j], gu_in_sem.at[j]) for j in range(2)]

    def s_save(m):
        return [pltpu.make_async_copy(s_out.at[j], s_all.at[m, j], s_sem.at[j]) for j in range(3)]

    def s_back(m):
        return [pltpu.make_async_copy(s_all.at[m, j], s_in.at[j], s_in_sem.at[j]) for j in range(3)]

    def forward(m):
        for p, r in enumerate(parts):
            h_came(m, p).wait()
            h = hb[m, r, :]
            wide, scale = scaled(h)
            a = (wide * scale).astype(BF)
            for n in tiles(ff):
                g, u = dot(a, wg[:, n]), dot(a, wu[:, n])
                gu[0, r, n] = g
                gu[1, r, n] = u
                s_out[2, r, n] = (g * jax.nn.sigmoid(g) * u).astype(BF)
            y = dot(s_out[2, r, :], wd[...]).astype(BF)
            ys[m % 2, r, :] = h + y
            onward(m, p).start()

    def by_hidden(d, g, u, r, n):
        by_hid = dot(d, wd[n, :], NT).astype(BF).astype(F32)
        s = jax.nn.sigmoid(g)
        sg = g * s
        s_out[2, r, n] = (sg * u).astype(BF)
        s_out[1, r, n] = (sg * by_hid).astype(BF)
        s_out[0, r, n] = (by_hid * u * (s + sg * (1.0 - s))).astype(BF)

    def by_input(m, r, d):
        da = dot(s_out[0, r, :], wg[...], NT).astype(BF) + dot(s_out[1, r, :], wu[...], NT).astype(BF)
        wide, scale = scaled(hb[m, r, :])
        da = da.astype(F32)
        c = jnp.sum(wide * da, -1, keepdims=True) * (scale * scale * scale) * (1.0 / hb.shape[2])
        dhs[m % 2, r, :] = d + (da * scale - wide * c).astype(BF)

    def backward(m):
        @pl.when(me == last)
        def _():
            for p, r in enumerate(parts):
                h_came(m, p).wait()
                d_came(m, p).wait()
                wide, scale = scaled(hb[m, r, :])
                a = (wide * scale).astype(BF)
                d = db[m, r, :]
                for n in tiles(ff):
                    by_hidden(d, dot(a, wg[:, n]), dot(a, wu[:, n]), r, n)
                by_input(m, r, d)
                back_again(m, p).start()

        @pl.when((me > 0) & (me < last))
        def _():
            for copy in gu_back(m):
                copy.wait()
            for p, r in enumerate(parts):
                d_came(m, p).wait()
                d = db[m, r, :]
                for n in tiles(ff):
                    by_hidden(d, gu_in[0, r, n], gu_in[1, r, n], r, n)
                by_input(m, r, d)
                back_again(m, p).start()

        @pl.when(me == 0)
        def _():
            for copy in gu_back(m):
                copy.wait()
            for p, r in enumerate(parts):
                d_came(m, p).wait()
                d = db[m, r, :]
                for n in tiles(ff):
                    by_hidden(d, gu_in[0, r, n], gu_in[1, r, n], r, n)

    def by_weights(m):
        for copy in s_back(m):
            copy.wait()
        wide, scale = scaled(hb[m])
        at[...] = (wide * scale).astype(BF).T
        dyt[...] = db[m].T
        for j, left in enumerate((at, at, dyt)):
            for n in tiles(ff):
                acc[j, :, n] += dot(left[...], s_in[j, :, n]).astype(BF).astype(F32)

    def step(t, carry):
        mb, mw = t - lead, t - lead - lag
        has_f = (me < last) & (t < micro)
        has_b = (mb >= 0) & (mb < micro)
        has_w = (mw >= 0) & (mw < micro)

        @pl.when((me < last) & (t >= 1) & (t <= micro))
        def _():
            for copy in gu_out(t - 1):
                copy.wait()

        @pl.when((mb >= 1) & (mb <= micro))
        def _():
            for copy in s_save(mb - 1):
                copy.wait()

        @pl.when(has_b & (me < last))
        def _():
            for copy in gu_back(mb):
                copy.start()

        @pl.when(has_w)
        def _():
            for copy in s_back(mw):
                copy.start()

        @pl.when(has_f & (t >= 2))
        def _():
            for p in range(PARTS):
                onward(t - 2, p).wait_send()

        @pl.when(has_f)
        def _():
            forward(t)
            for copy in gu_out(t):
                copy.start()

        @pl.when(has_b & (me > 0) & (mb >= 2))
        def _():
            for p in range(PARTS):
                back_again(mb - 2, p).wait_send()

        @pl.when(has_b)
        def _():
            backward(mb)
            for copy in s_save(mb):
                copy.start()

        @pl.when(has_w)
        def _():
            by_weights(mw)

        return carry

    lax.fori_loop(0, micro + lead + lag, step, 0)

    out = [pltpu.make_async_copy(s_in.at[j], o, o_sem.at[j]) for j, o in enumerate((og, ou, od))]
    for j in range(3):
        s_in[j] = acc[j].astype(BF)
        out[j].start()

    @pl.when(me < last)
    def _():
        for m in (micro - 2, micro - 1):
            for p in range(PARTS):
                onward(m, p).wait_send()

    @pl.when(me > 0)
    def _():
        for m in (micro - 2, micro - 1):
            for p in range(PARTS):
                back_again(m, p).wait_send()

    for copy in out:
        copy.wait()


def solution(mesh):
    stages = mesh.shape["pp"]

    def step(x, dy, wg, wu, wd):
        micro, tokens, d = x.shape
        ff = wg.shape[2]
        vmem, dma = pltpu.VMEM, pltpu.SemaphoreType.DMA
        wide = jax.ShapeDtypeStruct((d, ff), BF)
        og, ou, od, _, _ = pl.pallas_call(
            functools.partial(kernel, stages),
            out_shape=(wide, wide, wide,
                       jax.ShapeDtypeStruct((micro, 2, tokens, ff), F32), jax.ShapeDtypeStruct((micro, 3, tokens, ff), BF)),
            in_specs=[pl.BlockSpec(memory_space=pl.ANY)] * 5,
            out_specs=[pl.BlockSpec(memory_space=pl.ANY)] * 5,
            scratch_shapes=[
                vmem((micro, tokens, d), BF), vmem((micro, tokens, d), BF),
                vmem((d, ff), BF), vmem((d, ff), BF), vmem((ff, d), BF),
                vmem((3, d, ff), F32),
                vmem((2, tokens, ff), F32), vmem((2, tokens, ff), F32),
                vmem((3, tokens, ff), BF), vmem((3, tokens, ff), BF),
                vmem((2, tokens, d), BF), vmem((2, tokens, d), BF),
                vmem((d, tokens), BF), vmem((d, tokens), BF),
                dma((micro, PARTS)), dma((micro, PARTS)), dma((2, PARTS)), dma((2, PARTS)),
                dma((3,)), dma((2,)), dma((2,)), dma((3,)), dma((3,)), dma((3,)),
            ],
            compiler_params=pltpu.CompilerParams(collective_id=0, has_side_effects=True, vmem_limit_bytes=67043328),
            name="pipeline",
        )(x, dy, wg[0], wu[0], wd[0])
        return og[None], ou[None], od.T[None]

    return jax.shard_map(
        step,
        mesh=mesh,
        in_specs=(P("rep", None, None),) * 2 + (P("pp", None, None),) * 3,
        out_specs=(P(("rep", "pp"), None, None),) * 3,
        check_vma=False,
    )
```

time: 1190 us -> 321 us (0.27)
  the two profiles are of different devices: /device:TPU:3 before, /device:TPU:1 now
where the time goes in v1:
time: 321 us
  Pallas kernels  313 us (98%)
  local copies, waits for them, and re-layouts  7.36 us (2%)
    pallas_call x1, Pallas kernels, step(): pl.pallas_call(functools.partial(kernel, stages), out_shape=(wide, wide,...  313 us
    unnamed x7, local copies, waits for them, and re-layouts  7.36 us

profile of v1, /device:TPU:1, one launch (start us, length us, event | category | flops | bytes accessed | tf_op | source)
XLA Modules:
  0.0 321.2 jit_solution(3995324456828949925)
XLA Ops:
  0.6 313.2 %pipeline.1 = (bf16[512,1792]{1,0:T(8,128)(2,1)}, bf16[512,1792]{1,0:T(8,128)(2,1)}, bf16[512,1792]{1,0:T(8,128)(2,1)}, f32[16,2,512,1792]{3,2,1,0:T(8,128)}, bf16[16,3,512,1792]{3,2,1,0:T(8,128)(2,1)}) custom-call(bf16[16,512,512]{2,1,0:T(8,128)(2,1)} %x.1, bf16[16,512,512]{2,1,0:T(8,128)(2,1)} %dy.1, bf16[512,1792]{1,0:T(8,128)(2,1)} %bitcast.11, ...), custom_call_target="tpu_custom_call" | custom-call | tf_op jit(solution)/shard_map/pipeline/pallas_call | solution.py:276
  313.9 0.0 copy-start.1
  313.9 4.0 %copy.8 = bf16[1,1792,512]{2,1,0:T(8,128)(2,1)} copy(bf16[1,1792,512]{1,2,0:T(8,128)(2,1)} %bitcast.10) | data formatting | bytes 3670016
  317.8 0.0 copy-done.1
  317.8 0.0 copy-start
  317.8 1.2 copy.11
  319.1 0.9 copy-done
  320.0 1.2 copy.12
Async XLA Ops:
  313.9 4.0 %copy-start.1 = (bf16[512,1792]{1,0:T(8,128)(2,1)S(1)}, bf16[512,1792]{1,0:T(8,128)(2,1)}, u32[]{:S(2)}) copy-start(bf16[512,1792]{1,0:T(8,128)(2,1)} %get-tuple-element.6) | copy-start | bytes 5505028
  317.8 2.2 copy-start

commit v2 on v1

v2 whole, which is shorter than its diff:
```python
import functools

import jax
import jax.numpy as jnp
from jax import lax
from jax.experimental import pallas as pl
from jax.experimental.pallas import tpu as pltpu
from jax.sharding import PartitionSpec as P

BF, F32 = jnp.bfloat16, jnp.float32
LEAD = (15, 13, 11, 10, 6, 5, 2, 0)
LAG = (2, 3, 5, 6, 9, 10, 10, 5)
VIA = range(3, 13)
VIA_SLOTS = 6
TILE = 256
PARTS = 2
NN = (((1,), (0,)), ((), ()))
NT = (((1,), (1,)), ((), ()))


def dot(a, b, dims=NN):
    return lax.dot_general(a, b, dims, preferred_element_type=F32)


def scaled(h):
    wide = h.astype(F32)
    return wide, lax.rsqrt(jnp.mean(wide * wide, -1, keepdims=True) + 1e-6)


def tiles(ff):
    return [pl.ds(n, TILE) for n in range(0, ff, TILE)]


def pick(me, values):
    out = jnp.int32(values[0])
    for i in range(1, len(values)):
        out = jnp.where(me == i, jnp.int32(values[i]), out)
    return out


def kernel(stages, x, dy, wg_in, wu_in, wd_in, og, ou, od, gu_all, s_all, *scratch):
    (hb, db, wg, wu, wd, acc, gu, gu_in, s_out, s_in, hid, via, ys, dhs, at, dyt,
     h_sem, d_sem, y_sent, dh_sent, w_sem, gu_sem, gu_in_sem, s_sem, s_in_sem, o_sem, via_sem, via_sent) = scratch
    micro, tokens, _ = hb.shape
    ff = wg.shape[1]
    rows = tokens // PARTS
    last = stages - 1
    me = lax.axis_index("pp")
    lead, lag = pick(me, LEAD), pick(me, LAG)
    parts = [pl.ds(p * rows, rows) for p in range(PARTS)]

    weights = [pltpu.make_async_copy(a, b, w_sem.at[j]) for j, (a, b) in enumerate(((wg_in, wg), (wu_in, wu), (wd_in, wd)))]
    for copy in weights:
        copy.start()

    @pl.when(me == 0)
    def _():
        for m in range(micro):
            for p, r in enumerate(parts):
                pltpu.make_async_copy(x.at[m, r], hb.at[m, r], h_sem.at[m, p]).start()

    @pl.when(me == last)
    def _():
        for m in range(micro):
            for p, r in enumerate(parts):
                pltpu.make_async_copy(dy.at[m, r], db.at[m, r], d_sem.at[m, p]).start()

    low, high = stages // 2 - 1, stages // 2
    peers = [(i, i + 1) for i in range(last)] + [(a, b) for a in (0, last) for b in (low, high)]
    barrier = pltpu.get_barrier_semaphore()
    for a, b in peers:
        for one, other in ((a, b), (b, a)):
            @pl.when(me == one)
            def _():
                pl.semaphore_signal(barrier, inc=1, device_id={"pp": other}, device_id_type=pl.DeviceIdType.MESH)

    acc[...] = jnp.zeros_like(acc)

    pl.semaphore_wait(barrier, pick(me, [sum(i in pair for pair in peers) for i in range(stages)]))

    for copy in weights:
        copy.wait()

    def onward(m, p):
        r = parts[p]
        return pltpu.make_async_remote_copy(
            src_ref=ys.at[m % 2, r], dst_ref=hb.at[m, r], send_sem=y_sent.at[m % 2, p], recv_sem=h_sem.at[m, p],
            device_id={"pp": me + 1}, device_id_type=pl.DeviceIdType.MESH)

    def back_again(m, p):
        r = parts[p]
        return pltpu.make_async_remote_copy(
            src_ref=dhs.at[m % 2, r], dst_ref=db.at[m, r], send_sem=dh_sent.at[m % 2, p], recv_sem=d_sem.at[m, p],
            device_id={"pp": me - 1}, device_id_type=pl.DeviceIdType.MESH)

    def remote(src, dst, sent, came, device):
        return pltpu.make_async_remote_copy(src_ref=src, dst_ref=dst, send_sem=sent, recv_sem=came,
                                            device_id={"pp": device}, device_id_type=pl.DeviceIdType.MESH)

    half = PARTS - 1

    def goes_via(m):
        return (m >= VIA.start) & (m < VIA.stop)

    def onward_via(m):
        return remote(ys.at[m % 2, parts[half]], via.at[m % VIA_SLOTS], y_sent.at[m % 2, half], via_sem.at[m % VIA_SLOTS], 0)

    def back_via(m):
        return remote(dhs.at[m % 2, parts[half]], via.at[m % VIA_SLOTS], dh_sent.at[m % 2, half], via_sem.at[m % VIA_SLOTS], last)

    def pass_onward(m):
        return remote(via.at[m % VIA_SLOTS], hb.at[m, parts[half]], via_sent, h_sem.at[m, half], high)

    def pass_back(m):
        return remote(via.at[m % VIA_SLOTS], db.at[m, parts[half]], via_sent, d_sem.at[m, half], low)

    def send(direct, indirect, m, p, at_stage):
        if p < half:
            direct(m, p).start()
            return
        other_way = (me == at_stage) & goes_via(m)

        @pl.when(other_way)
        def _():
            indirect(m).start()

        @pl.when(jnp.logical_not(other_way))
        def _():
            direct(m, p).start()

    def h_came(m, p):
        r = parts[p]
        return pltpu.make_async_copy(x.at[m, r], hb.at[m, r], h_sem.at[m, p])

    def d_came(m, p):
        r = parts[p]
        return pltpu.make_async_copy(dy.at[m, r], db.at[m, r], d_sem.at[m, p])

    def gu_out(m, p):
        return pltpu.make_async_copy(gu.at[:, parts[p]], gu_all.at[m, :, parts[p]], gu_sem.at[p])

    def gu_back(m, p):
        return pltpu.make_async_copy(gu_all.at[m, :, parts[p]], gu_in.at[:, parts[p]], gu_in_sem.at[p])

    def s_save(m, p):
        return pltpu.make_async_copy(s_out.at[:, parts[p]], s_all.at[m, :, parts[p]], s_sem.at[p])

    def s_back(m, j):
        return pltpu.make_async_copy(s_all.at[m, j], s_in.at[j], s_in_sem.at[j])

    def forward(m):
        @pl.when(m >= 1)
        def _():
            for p in range(PARTS):
                gu_out(m - 1, p).wait()

        @pl.when(m >= 2)
        def _():
            for p in range(PARTS):
                onward(m - 2, p).wait_send()

        for p, r in enumerate(parts):
            h_came(m, p).wait()
            h = hb[m, r, :]
            wide, scale = scaled(h)
            a = (wide * scale).astype(BF)
            for n in tiles(ff):
                g, u = dot(a, wg[:, n]), dot(a, wu[:, n])
                gu[0, r, n] = g
                gu[1, r, n] = u
                hid[p % 2, :, n] = (g * jax.nn.sigmoid(g) * u).astype(BF)
            y = dot(hid[p % 2], wd[...]).astype(BF)
            ys[m % 2, r, :] = h + y
            send(onward, onward_via, m, p, low)
            gu_out(m, p).start()

    def by_hidden(d, g, u, r, n):
        by_hid = dot(d, wd[n, :], NT).astype(BF).astype(F32)
        s = jax.nn.sigmoid(g)
        sg = g * s
        s_out[2, r, n] = (sg * u).astype(BF)
        s_out[1, r, n] = (sg * by_hid).astype(BF)
        s_out[0, r, n] = (by_hid * u * (s + sg * (1.0 - s))).astype(BF)

    def by_input(m, r, d):
        da = dot(s_out[0, r, :], wg[...], NT).astype(BF) + dot(s_out[1, r, :], wu[...], NT).astype(BF)
        wide, scale = scaled(hb[m, r, :])
        da = da.astype(F32)
        c = jnp.sum(wide * da, -1, keepdims=True) * (scale * scale * scale) * (1.0 / hb.shape[2])
        dhs[m % 2, r, :] = d + (da * scale - wide * c).astype(BF)

    def backward_part(m, p, first, final):
        r = parts[p]
        d_came(m, p).wait()
        d = db[m, r, :]
        if final:
            h_came(m, p).wait()
            wide, scale = scaled(hb[m, r, :])
            a = (wide * scale).astype(BF)
            for n in tiles(ff):
                by_hidden(d, dot(a, wg[:, n]), dot(a, wu[:, n]), r, n)
        else:
            gu_back(m, p).wait()
            for n in tiles(ff):
                by_hidden(d, gu_in[0, r, n], gu_in[1, r, n], r, n)
        if not first:
            by_input(m, r, d)
            send(back_again, back_via, m, p, high)
        s_save(m, p).start()
        if not final:
            gu_back(jnp.minimum(m + 1, micro - 1), p).start()

    def backward(m):
        for first, final, here in ((True, False, me == 0), (False, False, (me > 0) & (me < last)), (False, True, me == last)):
            @pl.when(here)
            def _():
                @pl.when(m >= 1)
                def _():
                    for p in range(PARTS):
                        s_save(m - 1, p).wait()

                if not first:
                    @pl.when(m >= 2)
                    def _():
                        for p in range(PARTS):
                            back_again(m - 2, p).wait_send()

                for p in range(PARTS):
                    backward_part(m, p, first, final)

    def by_weights(m):
        for j in range(3):
            s_back(m, j).wait()
        dyt[...] = db[m].T
        wide, scale = scaled(hb[m])
        at[...] = (wide * scale).astype(BF).T
        for j, left in ((2, dyt), (0, at), (1, at)):
            for n in tiles(ff):
                acc[j, :, n] += dot(left[...], s_in[j, :, n]).astype(BF).astype(F32)
        for j in range(3):
            s_back(jnp.minimum(m + 1, micro - 1), j).start()

    def step(t, carry):
        mb, mw = t - lead, t - lead - lag
        passed = t - VIA_SLOTS

        @pl.when((me == 0) & goes_via(passed))
        def _():
            pass_onward(passed).wait_send()

        @pl.when((me == last) & goes_via(passed))
        def _():
            pass_back(passed).wait_send()

        @pl.when((me == 0) & goes_via(passed + 1))
        def _():
            onward_via(passed + 1).wait_recv()
            pass_onward(passed + 1).start()

        @pl.when((me == last) & goes_via(passed + 1))
        def _():
            back_via(passed + 1).wait_recv()
            pass_back(passed + 1).start()

        @pl.when((me < last) & (t == micro))
        def _():
            for p in range(PARTS):
                gu_out(micro - 1, p).wait()

        @pl.when(mb == micro)
        def _():
            for p in range(PARTS):
                s_save(micro - 1, p).wait()

        @pl.when((me < last) & (mb == micro))
        def _():
            for p in range(PARTS):
                gu_back(micro - 1, p).wait()

        @pl.when((me < last) & (mb == 0))
        def _():
            for p in range(PARTS):
                gu_back(0, p).start()

        @pl.when(mw == 0)
        def _():
            for j in range(3):
                s_back(0, j).start()

        @pl.when((me < last) & (t < micro))
        def _():
            forward(t)

        @pl.when((mb >= 0) & (mb < micro))
        def _():
            backward(mb)

        @pl.when((mw >= 0) & (mw < micro))
        def _():
            by_weights(mw)

        return carry

    lax.fori_loop(0, micro + lead + lag, step, 0)

    for j in range(3):
        s_back(micro - 1, j).wait()

    out = [pltpu.make_async_copy(s_in.at[j], o, o_sem.at[j]) for j, o in enumerate((og, ou, od))]
    for j in range(3):
        s_in[j] = acc[j].astype(BF)
        out[j].start()

    @pl.when(me < last)
    def _():
        for m in (micro - 2, micro - 1):
            for p in range(PARTS):
                onward(m, p).wait_send()

    @pl.when(me > 0)
    def _():
        for m in (micro - 2, micro - 1):
            for p in range(PARTS):
                back_again(m, p).wait_send()

    for copy in out:
        copy.wait()


def solution(mesh):
    stages = mesh.shape["pp"]

    def step(x, dy, wg, wu, wd):
        micro, tokens, d = x.shape
        ff = wg.shape[2]
        vmem, dma = pltpu.VMEM, pltpu.SemaphoreType.DMA
        wide = jax.ShapeDtypeStruct((d, ff), BF)
        og, ou, od, _, _ = pl.pallas_call(
            functools.partial(kernel, stages),
            out_shape=(wide, wide, wide,
                       jax.ShapeDtypeStruct((micro, 2, tokens, ff), F32), jax.ShapeDtypeStruct((micro, 3, tokens, ff), BF)),
            in_specs=[pl.BlockSpec(memory_space=pl.ANY)] * 5,
            out_specs=[pl.BlockSpec(memory_space=pl.ANY)] * 5,
            scratch_shapes=[
                vmem((micro, tokens, d), BF), vmem((micro, tokens, d), BF),
                vmem((d, ff), BF), vmem((d, ff), BF), vmem((ff, d), BF),
                vmem((3, d, ff), F32),
                vmem((2, tokens, ff), F32), vmem((2, tokens, ff), F32),
                vmem((3, tokens, ff), BF), vmem((3, tokens, ff), BF), vmem((2, tokens // PARTS, ff), BF), vmem((VIA_SLOTS, tokens // PARTS, d), BF),
                vmem((2, tokens, d), BF), vmem((2, tokens, d), BF),
                vmem((d, tokens), BF), vmem((d, tokens), BF),
                dma((micro, PARTS)), dma((micro, PARTS)), dma((2, PARTS)), dma((2, PARTS)),
                dma((3,)), dma((PARTS,)), dma((PARTS,)), dma((PARTS,)), dma((3,)), dma((3,)), dma((VIA_SLOTS,)), dma,
            ],
            compiler_params=pltpu.CompilerParams(collective_id=0, has_side_effects=True, vmem_limit_bytes=67043328),
            name="pipeline",
        )(x, dy, wg[0], wu[0], wd[0])
        return og[None], ou[None], od.T[None]

    return jax.shard_map(
        step,
        mesh=mesh,
        in_specs=(P("rep", None, None),) * 2 + (P("pp", None, None),) * 3,
        out_specs=(P(("rep", "pp"), None, None),) * 3,
        check_vma=False,
    )
```

time: 321 us -> 269 us (0.84)
  the two profiles are of different devices: /device:TPU:1 before, /device:TPU:3 now
where the time goes in v2:
time: 269 us
  Pallas kernels  261 us (97%)
  local copies, waits for them, and re-layouts  7.36 us (3%)
    pallas_call x1, Pallas kernels, step(): pl.pallas_call(functools.partial(kernel, stages), out_shape=(wide, wide,...  261 us
    unnamed x7, local copies, waits for them, and re-layouts  7.36 us

profile of v2, /device:TPU:3, one launch (start us, length us, event | category | flops | bytes accessed | tf_op | source)
XLA Modules:
  0.0 269.2 jit_solution(15686579088260939476)
XLA Ops:
  0.6 261.2 %pipeline.1 = (bf16[512,1792]{1,0:T(8,128)(2,1)}, bf16[512,1792]{1,0:T(8,128)(2,1)}, bf16[512,1792]{1,0:T(8,128)(2,1)}, f32[16,2,512,1792]{3,2,1,0:T(8,128)}, bf16[16,3,512,1792]{3,2,1,0:T(8,128)(2,1)}) custom-call(bf16[16,512,512]{2,1,0:T(8,128)(2,1)} %x.1, bf16[16,512,512]{2,1,0:T(8,128)(2,1)} %dy.1, bf16[512,1792]{1,0:T(8,128)(2,1)} %bitcast.11, ...), custom_call_target="tpu_custom_call" | custom-call | tf_op jit(solution)/shard_map/pipeline/pallas_call | solution.py:338
  261.8 0.0 copy-start.1
  261.8 4.0 %copy.8 = bf16[1,1792,512]{2,1,0:T(8,128)(2,1)} copy(bf16[1,1792,512]{1,2,0:T(8,128)(2,1)} %bitcast.10) | data formatting | bytes 3670016
  265.8 0.0 copy-done.1
  265.8 0.0 copy-start
  265.8 1.2 copy.11
  267.0 0.9 copy-done
  267.9 1.2 copy.12
Async XLA Ops:
  261.8 4.0 %copy-start.1 = (bf16[512,1792]{1,0:T(8,128)(2,1)S(1)}, bf16[512,1792]{1,0:T(8,128)(2,1)}, u32[]{:S(2)}) copy-start(bf16[512,1792]{1,0:T(8,128)(2,1)} %get-tuple-element.6) | copy-start | bytes 5505028
  265.8 2.2 copy-start

commit v3 on v2

--- a/solution.py
+++ b/solution.py
@@ -8,8 +8,8 @@
 from jax.sharding import PartitionSpec as P
 
 BF, F32 = jnp.bfloat16, jnp.float32
-LEAD = (15, 13, 11, 10, 6, 5, 2, 0)
-LAG = (2, 3, 5, 6, 9, 10, 10, 5)
+LEAD = (14, 13, 11, 10, 6, 5, 2, 0)
+LAG = (2, 3, 5, 6, 9, 10, 11, 6)
 VIA = range(3, 13)
 VIA_SLOTS = 6
 TILE = 256
@@ -149,11 +149,6 @@
         return pltpu.make_async_copy(s_all.at[m, j], s_in.at[j], s_in_sem.at[j])
 
     def forward(m):
-        @pl.when(m >= 1)
-        def _():
-            for p in range(PARTS):
-                gu_out(m - 1, p).wait()
-
         @pl.when(m >= 2)
         def _():
             for p in range(PARTS):
@@ -262,10 +257,10 @@
             back_via(passed + 1).wait_recv()
             pass_back(passed + 1).start()
 
-        @pl.when((me < last) & (t == micro))
-        def _():
-            for p in range(PARTS):
-                gu_out(micro - 1, p).wait()
+        @pl.when((me < last) & (t >= 1) & (t <= micro))
+        def _():
+            for p in range(PARTS):
+                gu_out(t - 1, p).wait()
 
         @pl.when(mb == micro)
         def _():
@@ -277,7 +272,7 @@
             for p in range(PARTS):
                 gu_back(micro - 1, p).wait()
 
-        @pl.when((me < last) & (mb == 0))
+        @pl.when((me < last) & (mb == -1))
         def _():
             for p in range(PARTS):
                 gu_back(0, p).start()
@@ -287,13 +282,13 @@
             for j in range(3):
                 s_back(0, j).start()
 
+        @pl.when((mb >= 0) & (mb < micro))
+        def _():
+            backward(mb)
+
         @pl.when((me < last) & (t < micro))
         def _():
             forward(t)
-
-        @pl.when((mb >= 0) & (mb < micro))
-        def _():
-            backward(mb)
 
         @pl.when((mw >= 0) & (mw < micro))
         def _():

time: 269 us -> 272 us (1.011)
  Pallas kernels: 261 us -> 264 us
where the time goes in v3:
time: 272 us
  Pallas kernels  264 us (97%)
  local copies, waits for them, and re-layouts  7.36 us (3%)
    pallas_call x1, Pallas kernels, step(): pl.pallas_call(functools.partial(kernel, stages), out_shape=(wide, wide,...  264 us
    unnamed x7, local copies, waits for them, and re-layouts  7.36 us

profile of v3, /device:TPU:3, one launch (start us, length us, event | category | flops | bytes accessed | tf_op | source)
XLA Modules:
  0.0 271.9 jit_solution(17431879320353754913)
XLA Ops:
  0.6 263.9 %pipeline.1 = (bf16[512,1792]{1,0:T(8,128)(2,1)}, bf16[512,1792]{1,0:T(8,128)(2,1)}, bf16[512,1792]{1,0:T(8,128)(2,1)}, f32[16,2,512,1792]{3,2,1,0:T(8,128)}, bf16[16,3,512,1792]{3,2,1,0:T(8,128)(2,1)}) custom-call(bf16[16,512,512]{2,1,0:T(8,128)(2,1)} %x.1, bf16[16,512,512]{2,1,0:T(8,128)(2,1)} %dy.1, bf16[512,1792]{1,0:T(8,128)(2,1)} %bitcast.11, ...), custom_call_target="tpu_custom_call" | custom-call | tf_op jit(solution)/shard_map/pipeline/pallas_call | solution.py:333
  264.5 0.0 copy-start.1
  264.5 4.0 %copy.8 = bf16[1,1792,512]{2,1,0:T(8,128)(2,1)} copy(bf16[1,1792,512]{1,2,0:T(8,128)(2,1)} %bitcast.10) | data formatting | bytes 3670016
  268.5 0.0 copy-done.1
  268.5 0.0 copy-start
  268.5 1.2 copy.11
  269.7 0.9 copy-done
  270.6 1.2 copy.12
Async XLA Ops:
  264.5 4.0 %copy-start.1 = (bf16[512,1792]{1,0:T(8,128)(2,1)S(1)}, bf16[512,1792]{1,0:T(8,128)(2,1)}, u32[]{:S(2)}) copy-start(bf16[512,1792]{1,0:T(8,128)(2,1)} %get-tuple-element.6) | copy-start | bytes 5505028
  268.5 2.2 copy-start

commit v4 on v2

--- a/solution.py
+++ b/solution.py
@@ -9,7 +9,7 @@
 
 BF, F32 = jnp.bfloat16, jnp.float32
 LEAD = (15, 13, 11, 10, 6, 5, 2, 0)
-LAG = (2, 3, 5, 6, 9, 10, 10, 5)
+LAG = (2, 2, 4, 5, 9, 10, 10, 4)
 VIA = range(3, 13)
 VIA_SLOTS = 6
 TILE = 256

time: 269 us -> 269 us (level)
  no operation moved by 1% of the time
where the time goes in v4:
time: 269 us
  Pallas kernels  261 us (97%)
  local copies, waits for them, and re-layouts  7.36 us (3%)
    pallas_call x1, Pallas kernels, step(): pl.pallas_call(functools.partial(kernel, stages), out_shape=(wide, wide,...  261 us
    unnamed x7, local copies, waits for them, and re-layouts  7.36 us

profile of v4, /device:TPU:3, one launch (start us, length us, event | category | flops | bytes accessed | tf_op | source)
XLA Modules:
  0.0 269.2 jit_solution(17994221059085078304)
XLA Ops:
  0.6 261.2 %pipeline.1 = (bf16[512,1792]{1,0:T(8,128)(2,1)}, bf16[512,1792]{1,0:T(8,128)(2,1)}, bf16[512,1792]{1,0:T(8,128)(2,1)}, f32[16,2,512,1792]{3,2,1,0:T(8,128)}, bf16[16,3,512,1792]{3,2,1,0:T(8,128)(2,1)}) custom-call(bf16[16,512,512]{2,1,0:T(8,128)(2,1)} %x.1, bf16[16,512,512]{2,1,0:T(8,128)(2,1)} %dy.1, bf16[512,1792]{1,0:T(8,128)(2,1)} %bitcast.11, ...), custom_call_target="tpu_custom_call" | custom-call | tf_op jit(solution)/shard_map/pipeline/pallas_call | solution.py:338
  261.8 0.0 copy-start.1
  261.8 4.0 %copy.8 = bf16[1,1792,512]{2,1,0:T(8,128)(2,1)} copy(bf16[1,1792,512]{1,2,0:T(8,128)(2,1)} %bitcast.10) | data formatting | bytes 3670016
  265.8 0.0 copy-done.1
  265.8 0.0 copy-start
  265.8 1.2 copy.11
  267.0 0.9 copy-done
  267.9 1.2 copy.12
Async XLA Ops:
  261.8 4.0 %copy-start.1 = (bf16[512,1792]{1,0:T(8,128)(2,1)S(1)}, bf16[512,1792]{1,0:T(8,128)(2,1)}, u32[]{:S(2)}) copy-start(bf16[512,1792]{1,0:T(8,128)(2,1)} %get-tuple-element.6) | copy-start | bytes 5505028
  265.8 2.2 copy-start
